TPU v7x, 256 devices: a whole 4x4x8 slice. The times are simulated.
256 devices in a mesh: pb: 64 (over x, y, z_hi, core), ga: 4 (over z_lo).
Axes of the slice: x: 4, y: 4, z: 8 (z_hi: 2, z_lo: 4; z = z_hi * 4 + z_lo), core: 2. Of those that a mesh axis runs over, the one named last changes fastest.
Arguments:
- query_points: float32 [3, 262144], P(None, 'pb'), may hold values from 0 to 1
- cotangent: bfloat16 [64, 262144], P(None, 'pb'), may hold values from -6 to 6
- slab_ids: int32 [8, 262144], P(None, 'pb'), may hold values from -1 to 3
- rel_cells: int32 [8, 262144], P(None, 'pb'), may hold values from 0 to 511
- offsets: int32 [4, 2048], P('ga', 'pb'), may hold values from 0 to 15872
- latent: bfloat16 [4, 64, 16384], P('ga', None, 'pb'), may hold values from -6 to 6
- w_in: float32 [80, 6], replicated, may hold values from -2.5 to 2.5
- b_in: float32 [80], replicated, may hold values from -3 to 3
- w_out: bfloat16 [64, 80], replicated, may hold values from -0.625 to 0.625
- b_out: float32 [64], replicated, may hold values from -3 to 3
Outputs:
- grid_grad: float32 [4, 64, 16384], P('ga', None, 'pb')
- w_in_grad: float32 [80, 6], replicated
- b_in_grad: float32 [80], replicated
- w_out_grad: float32 [64, 80], replicated
- b_out_grad: float32 [64], replicated
Inputs may be any that keep to these rules, and one draw needn't show every extreme that they name: `slab_ids`: -1 marks a padding slot; otherwise the slab that holds the neighbour cell.
All inputs are finite; a program needn't handle non-finite values.
Results may differ from a plain program's by a relative error of at most 0.0085.
Values may be sent and summed in bfloat16 or wider, within the bound.
A program may use at most 64 MiB of HBM per device.

v0:
```python
import functools
import math
import jax
import jax.numpy as jnp
from jax import lax
from jax.sharding import Mesh
from jax.sharding import PartitionSpec as P

KN = 8
TILE = 128
WIN = 512
GX = 64
ZS = 4
PB = ("pb_0", "pb_1", "pb_2", "pb_3")
PB_GA = ("pb_0", "pb_1", "pb_2", "pb_3", "ga")


def cut_along(value, dim, length):
    before, after = (value.shape[:dim], value.shape[dim + 1 :])
    return jnp.moveaxis(value.reshape(*before, length, -1, *after), dim, 0)


def sum_at_owner(value, axis, dim):
    tiles = cut_along(value, dim, lax.axis_size(axis))
    arrived = lax.all_to_all(tiles, axis, split_axis=0, concat_axis=0, tiled=True)
    return arrived.astype(jnp.float32).sum(axis=0)


def by_axis(value, axes):
    return functools.reduce(lax.psum, axes, value)


def gelu_exact(values):
    return jax.nn.gelu(values, approximate=False)


def shards(query_points, cotangent, slab_ids, rel_cells, offsets, latent, w_in, b_in, w_out, b_out):
    channels = latent.shape[1]
    slab_feats = lax.all_gather(latent, PB, axis=2, tiled=True)[0]
    cells_slab = slab_feats.shape[1]
    slab_here = lax.axis_index("ga")
    queries_dev = query_points.shape[1]
    tiles_dev = queries_dev // TILE
    per_block = math.gcd(tiles_dev, 4)
    blocks = tiles_dev // per_block
    entries = KN * TILE

    def reshape_tiles(values):
        leading = values.shape[0]
        return values.reshape(leading, blocks, per_block, TILE).transpose(1, 2, 0, 3)

    def tile_work(anchor, points, cot_cols, slabs, rels):
        window = lax.dynamic_slice_in_dim(slab_feats, anchor, WIN, 1)
        rel_flat = rels.reshape(-1)
        live_flat = slabs.reshape(-1) == slab_here
        onehot = (
            (lax.broadcasted_iota(jnp.int32, (WIN, entries), 0) == rel_flat[None, :])
            & live_flat[None, :]
        ).astype(jnp.bfloat16)
        feats = jnp.dot(window, onehot, preferred_element_type=jnp.float32)
        cell = anchor + rel_flat
        along_x = cell // (GX * ZS)
        along_y = cell // ZS % GX
        along_z = cell % ZS + slab_here * ZS
        centres = jnp.stack(
            [
                (along_x.astype(jnp.float32) + 0.5) / GX,
                (along_y.astype(jnp.float32) + 0.5) / GX,
                (along_z.astype(jnp.float32) + 0.5) / GX,
            ],
            0,
        )
        features_in = jnp.concatenate([jnp.tile(points, (1, KN)), centres], 0)
        mask_flat = live_flat.astype(jnp.float32)
        cot_flat = jnp.tile(cot_cols.astype(jnp.float32), (1, KN))
        preact = (
            jnp.dot(
                w_in,
                features_in,
                precision=lax.Precision.HIGHEST,
                preferred_element_type=jnp.float32,
            )
            + b_in[:, None]
        )
        hidden = gelu_exact(preact).astype(jnp.bfloat16)
        kernel = jnp.dot(w_out, hidden, preferred_element_type=jnp.float32) + b_out[:, None]
        grad_cell = (kernel * cot_flat * mask_flat).astype(jnp.bfloat16)
        grad_kernel = (feats * cot_flat * mask_flat).astype(jnp.bfloat16)
        window_grad = lax.dot_general(
            grad_cell, onehot, (((1,), (1,)), ((), ())), preferred_element_type=jnp.float32
        )
        grad_w_out = lax.dot_general(
            grad_kernel, hidden, (((1,), (1,)), ((), ())), preferred_element_type=jnp.float32
        )
        grad_b_out = jnp.sum(grad_kernel.astype(jnp.float32), 1)
        grad_hidden = lax.dot_general(
            w_out, grad_kernel, (((0,), (0,)), ((), ())), preferred_element_type=jnp.float32
        )
        grad_pre = jax.vjp(gelu_exact, preact)[1](grad_hidden)[0]
        grad_w_in = lax.dot_general(
            grad_pre,
            features_in,
            (((1,), (1,)), ((), ())),
            precision=lax.Precision.HIGHEST,
            preferred_element_type=jnp.float32,
        )
        grad_b_in = jnp.sum(grad_pre, 1)
        return (window_grad, grad_w_in, grad_b_in, grad_w_out, grad_b_out)

    def advance(running, inputs_block):
        partial_grad, totals = running
        anchors, points, cot_cols, slabs, rels = inputs_block
        results = jax.vmap(tile_work)(anchors, points, cot_cols, slabs, rels)
        for number in range(per_block):
            current = lax.dynamic_slice_in_dim(partial_grad, anchors[number], WIN, 1)
            partial_grad = lax.dynamic_update_slice_in_dim(
                partial_grad, current + results[0][number], anchors[number], 1
            )
        totals = tuple((old + jnp.sum(new, 0) for old, new in zip(totals, results[1:])))
        return ((partial_grad, totals), None)

    start_totals = (
        jnp.zeros((w_in.shape[0], 6), jnp.float32),
        jnp.zeros((w_in.shape[0],), jnp.float32),
        jnp.zeros((channels, w_in.shape[0]), jnp.float32),
        jnp.zeros((channels,), jnp.float32),
    )
    start_grid = jnp.zeros((channels, cells_slab), jnp.float32)
    inputs_all = (
        offsets[0].reshape(blocks, per_block),
        reshape_tiles(query_points),
        reshape_tiles(cotangent),
        reshape_tiles(slab_ids),
        reshape_tiles(rel_cells),
    )
    (partial_grad, totals), _ = lax.scan(advance, (start_grid, start_totals), inputs_all)
    owned = sum_at_owner(partial_grad.astype(jnp.bfloat16), PB, 1)
    sums = (
        by_axis(totals[0], PB_GA),
        by_axis(totals[1], PB_GA),
        by_axis(totals[2], PB_GA),
        by_axis(totals[3], PB_GA),
    )
    scale = float(queries_dev * lax.axis_size(PB)) ** (-0.5)
    return (owned[None], sums[0] * scale, sums[1] * scale, sums[2] * scale, sums[3] * scale)


def solution(mesh):
    finer = Mesh(
        mesh.devices.reshape(4, 4, 2, 2, mesh.shape["ga"]), ("pb_0", "pb_1", "pb_2", "pb_3", "ga")
    )
    in_specs = (
        P(None, PB),
        P(None, PB),
        P(None, PB),
        P(None, PB),
        P("ga", PB),
        P("ga", None, PB),
        P(),
        P(),
        P(),
        P(),
    )
    out_specs = (P("ga", None, PB), P(), P(), P(), P())
    return jax.shard_map(
        shards, mesh=finer, in_specs=in_specs, out_specs=out_specs, check_vma=False
    )
```

profile of v0, /device:TPU:2, one launch (start us, length us, event | category | flops | bytes accessed | tf_op | source)
XLA Modules:
  0.0 575.7 jit_solution(1907002252681811050)
XLA Ops:
  13.0 86.1 %all-gather.2.cloned.1.call-done = bf16[1,64,16384]{2,1,0:T(8,128)(2,1)} async-done(((bf16[1,64,256]{2,1,0:T(8,128)(2,1)}), bf16[1,64,16384]{2,1,0:T(8,128)(2,1)}) %all-gather.2.cloned.1.call-update) | async-done | bytes 2097168 | tf_op jit(solution)/shard_map/all_gather | solution.py:39
  101.4 365.0 %while.26 = (s32[]{:T(128)}, f32[64,16384]{1,0:T(8,128)}, f32[80,6]{0,1:T(8,128)S(1)}, f32[80]{0:T(128)S(1)}, f32[64,80]{1,0:T(8,128)S(1)}, /*index=5*/f32[64]{0...) while((s32[]{:T(128)}, f32[64,16384]{1,0:T(8,128)}, ...), condition=%wide.region_3.4_spmd.clone, body=%wide.region_0.3_spmd.clone.sunk | while | flops 747289728 | bytes 21654660 | solution.py:136
  112.4 8.9 %while.27 = (s32[]{:T(128)}, bf16[64,16384]{1,0:T(8,128)(2,1)}, s32[4,2]{0,1:T(2,128)S(1)}, bf16[4,64,512]{2,1,0:T(8,128)(2,1)S(1)}, s32[]{:T(128)}) while((s32[]{:T(128)}, bf16[64,16384]{1,0:T(8,128)(2,1)}, s32[4,2]{0,1:T(2,128)S(1)}, bf16[4,64,512]{2,1,0:T(8,128)(2,1)S(1)}, s32[]{:T(128)}) %tuple.83), condition=%wide.while_cond, body=%wide.while_body.sunk | while | flops 2 | bytes 131177 | solution.py:53
  123.8 5.4 fusion.121
  131.4 2.6 fusion.128
  158.0 8.9 %while.27 = (s32[]{:T(128)}, bf16[64,16384]{1,0:T(8,128)(2,1)}, s32[4,2]{0,1:T(2,128)S(1)}, bf16[4,64,512]{2,1,0:T(8,128)(2,1)S(1)}, s32[]{:T(128)}) while((s32[]{:T(128)}, bf16[64,16384]{1,0:T(8,128)(2,1)}, s32[4,2]{0,1:T(2,128)S(1)}, bf16[4,64,512]{2,1,0:T(8,128)(2,1)S(1)}, s32[]{:T(128)}) %tuple.83), condition=%wide.while_cond, body=%wide.while_body.sunk | while | flops 2 | bytes 131177 | solution.py:53
  169.4 5.4 fusion.121
  177.0 2.6 fusion.128
  203.6 8.9 %while.27 = (s32[]{:T(128)}, bf16[64,16384]{1,0:T(8,128)(2,1)}, s32[4,2]{0,1:T(2,128)S(1)}, bf16[4,64,512]{2,1,0:T(8,128)(2,1)S(1)}, s32[]{:T(128)}) while((s32[]{:T(128)}, bf16[64,16384]{1,0:T(8,128)(2,1)}, s32[4,2]{0,1:T(2,128)S(1)}, bf16[4,64,512]{2,1,0:T(8,128)(2,1)S(1)}, s32[]{:T(128)}) %tuple.83), condition=%wide.while_cond, body=%wide.while_body.sunk | while | flops 2 | bytes 131177 | solution.py:53
  215.0 5.4 fusion.121
  222.7 2.6 fusion.128
  249.2 8.9 %while.27 = (s32[]{:T(128)}, bf16[64,16384]{1,0:T(8,128)(2,1)}, s32[4,2]{0,1:T(2,128)S(1)}, bf16[4,64,512]{2,1,0:T(8,128)(2,1)S(1)}, s32[]{:T(128)}) while((s32[]{:T(128)}, bf16[64,16384]{1,0:T(8,128)(2,1)}, s32[4,2]{0,1:T(2,128)S(1)}, bf16[4,64,512]{2,1,0:T(8,128)(2,1)S(1)}, s32[]{:T(128)}) %tuple.83), condition=%wide.while_cond, body=%wide.while_body.sunk | while | flops 2 | bytes 131177 | solution.py:53
  260.6 5.4 fusion.121
  268.3 2.6 fusion.128
  294.8 8.9 %while.27 = (s32[]{:T(128)}, bf16[64,16384]{1,0:T(8,128)(2,1)}, s32[4,2]{0,1:T(2,128)S(1)}, bf16[4,64,512]{2,1,0:T(8,128)(2,1)S(1)}, s32[]{:T(128)}) while((s32[]{:T(128)}, bf16[64,16384]{1,0:T(8,128)(2,1)}, s32[4,2]{0,1:T(2,128)S(1)}, bf16[4,64,512]{2,1,0:T(8,128)(2,1)S(1)}, s32[]{:T(128)}) %tuple.83), condition=%wide.while_cond, body=%wide.while_body.sunk | while | flops 2 | bytes 131177 | solution.py:53
  306.3 5.4 fusion.121
  313.9 2.6 fusion.128
  340.5 8.9 %while.27 = (s32[]{:T(128)}, bf16[64,16384]{1,0:T(8,128)(2,1)}, s32[4,2]{0,1:T(2,128)S(1)}, bf16[4,64,512]{2,1,0:T(8,128)(2,1)S(1)}, s32[]{:T(128)}) while((s32[]{:T(128)}, bf16[64,16384]{1,0:T(8,128)(2,1)}, s32[4,2]{0,1:T(2,128)S(1)}, bf16[4,64,512]{2,1,0:T(8,128)(2,1)S(1)}, s32[]{:T(128)}) %tuple.83), condition=%wide.while_cond, body=%wide.while_body.sunk | while | flops 2 | bytes 131177 | solution.py:53
  351.9 5.4 fusion.121
  359.6 2.6 fusion.128
  386.1 8.9 %while.27 = (s32[]{:T(128)}, bf16[64,16384]{1,0:T(8,128)(2,1)}, s32[4,2]{0,1:T(2,128)S(1)}, bf16[4,64,512]{2,1,0:T(8,128)(2,1)S(1)}, s32[]{:T(128)}) while((s32[]{:T(128)}, bf16[64,16384]{1,0:T(8,128)(2,1)}, s32[4,2]{0,1:T(2,128)S(1)}, bf16[4,64,512]{2,1,0:T(8,128)(2,1)S(1)}, s32[]{:T(128)}) %tuple.83), condition=%wide.while_cond, body=%wide.while_body.sunk | while | flops 2 | bytes 131177 | solution.py:53
  397.6 5.4 fusion.121
  405.2 2.6 fusion.128
  431.8 8.9 %while.27 = (s32[]{:T(128)}, bf16[64,16384]{1,0:T(8,128)(2,1)}, s32[4,2]{0,1:T(2,128)S(1)}, bf16[4,64,512]{2,1,0:T(8,128)(2,1)S(1)}, s32[]{:T(128)}) while((s32[]{:T(128)}, bf16[64,16384]{1,0:T(8,128)(2,1)}, s32[4,2]{0,1:T(2,128)S(1)}, bf16[4,64,512]{2,1,0:T(8,128)(2,1)S(1)}, s32[]{:T(128)}) %tuple.83), condition=%wide.while_cond, body=%wide.while_body.sunk | while | flops 2 | bytes 131177 | solution.py:53
  443.2 5.4 fusion.121
  450.8 2.6 fusion.128
  471.9 6.8 %all-to-all-start = ((bf16[64,64,256]{2,1,0:T(8,128)(2,1)}), bf16[64,64,256]{2,1,0:T(8,128)(2,1)S(1)}, u32[]{:S(2)}, u32[]{:S(2)}) async-start(bf16[64,64,256]{2,1,0:T(8,128)(2,1)} %copy.31), calls=%async_computation | async-start | bytes 4194304 | tf_op jit(solution)/shard_map/all_to_all | solution.py:25
  478.7 29.5 %all-reduce.3 = (f32[80,6]{0,1:T(8,128)S(1)}, f32[80]{0:T(128)S(1)}, f32[64,80]{1,0:T(8,128)S(1)}, f32[64]{0:T(128)S(1)}) all-reduce(f32[80,6]{0,1:T(8,128)S(1)} %get-tuple-element.285, f32[80]{0:T(128)S(1)} %get-tuple-element.286, ...), channel_id=1, replica_groups=mesh['pb_0'=4,'pb_1'=4,'pb_2'=2,'pb_3'=2,'ga'=4] {'pb_0'}, use_global_device_ids=true, to_apply=%region_5.6 | all-reduce | flops 5744 | bytes 45952 | tf_op jit(solution)/shard_map/psum | solution.py:30
  508.2 17.2 %all-reduce.2 = (f32[80,6]{0,1:T(8,128)S(1)}, f32[80]{0:T(128)S(1)}, f32[64,80]{1,0:T(8,128)S(1)}, f32[64]{0:T(128)S(1)}) all-reduce(f32[80,6]{0,1:T(8,128)S(1)} %get-tuple-element.497, f32[80]{0:T(128)S(1)} %get-tuple-element.498, ...), channel_id=1, replica_groups=mesh['pb_0'=4,'pb_1'=4,'pb_2'=2,'pb_3'=2,'ga'=4] {'pb_1'}, use_global_device_ids=true, to_apply=%region_6.7 | all-reduce | flops 5744 | bytes 45952 | tf_op jit(solution)/shard_map/psum | solution.py:30
  525.4 20.7 %all-reduce.5 = (f32[80,6]{0,1:T(8,128)S(1)}, f32[80]{0:T(128)S(1)}, f32[64,80]{1,0:T(8,128)S(1)}, f32[64]{0:T(128)S(1)}) all-reduce(f32[80,6]{0,1:T(8,128)S(1)} %get-tuple-element.493, f32[80]{0:T(128)S(1)} %get-tuple-element.494, ...), channel_id=1, replica_groups=mesh['pb_0'=4,'pb_1'=4,'pb_2'=2,'pb_3'=2,'ga'=4] {'pb_2'}, use_global_device_ids=true, to_apply=%region_7.8 | all-reduce | flops 5744 | bytes 45952 | tf_op jit(solution)/shard_map/psum | solution.py:30
  546.1 3.5 all-reduce.4
  549.6 16.1 %all-reduce.1 = (f32[80,6]{0,1:T(8,128)S(1)}, f32[80]{0:T(128)S(1)}, f32[64,80]{1,0:T(8,128)S(1)}, f32[64]{0:T(128)S(1)}) all-reduce(f32[80,6]{0,1:T(8,128)S(1)} %get-tuple-element.501, f32[80]{0:T(128)S(1)} %get-tuple-element.502, ...), channel_id=1, replica_groups=mesh['pb_0'=4,'pb_1'=4,'pb_2'=2,'pb_3'=2,'ga'=4] {'ga'}, use_global_device_ids=true, to_apply=%region_9.10 | all-reduce | flops 5744 | bytes 45952 | tf_op jit(solution)/shard_map/psum | solution.py:30
  (389 shorter events, 255.1 us)
Async XLA Ops:
  7.2 91.9 %all-gather.2.cloned.1.call-start = ((), (), s32[]{:S(2)}) async-start(), calls=%async_computation.1 | async-start | bytes 2129920 | tf_op jit(solution)/shard_map/all_gather | solution.py:39
  99.1 2.3 copy-start
  99.1 2.3 copy-start.1
  99.1 2.3 copy-start.2
  99.1 2.3 copy-start.3
  471.9 96.0 %all-to-all-start = ((bf16[64,64,256]{2,1,0:T(8,128)(2,1)}), bf16[64,64,256]{2,1,0:T(8,128)(2,1)S(1)}, u32[]{:S(2)}, u32[]{:S(2)}) async-start(bf16[64,64,256]{2,1,0:T(8,128)(2,1)} %copy.31), calls=%async_computation | async-start | bytes 4194304 | tf_op jit(solution)/shard_map/all_to_all | solution.py:25
Sparse Core Ops, SparseCore 0:
  11.3 87.7 all-gather.1
where the time goes:
time: 581 us; the launch traced here: 576 us
  local copies, waits for them, and re-layouts  159 us (27%)
  matrix products  111 us (19%)
  blocking collectives  87 us (15%)
  waiting for transfers between devices  86.8 us (15%)
  loops' own time  63.4 us (11%)
  other arithmetic  47.1 us (8%)
  between operations  14.1 us (2%)
  starting transfers between devices  6.81 us (1%)
    psum x5, blocking collectives, by_axis(): return functools.reduce(lax.psum, axes, value)  87 us
    all_gather x1, waiting for transfers between devices, shards(): slab_feats = lax.all_gather(latent, PB, axis=2, tiled=True)[0]  86.1 us
    gather x96, local copies, waits for them, and re-layouts  70.8 us
    another operation x1, loops' own time, shards(): lax.scan(advance, (start_grid, start_totals), inputs_all)  62.7 us
    dynamic_update_slice x32, local copies, waits for them, and re-layouts, advance(): lax.dynamic_update_slice_in_dim(partial_grad, current + results[0][number...  59.4 us
    dot_general x8, matrix products, tile_work(): jnp.dot(w_in, features_in, precision=lax.Precision.HIGHEST, preferred_ele...  42.8 us
    add x32, other arithmetic, advance(): current + results[0][number]  32.5 us
    dot_general x8, matrix products, tile_work(): lax.dot_general(w_out, grad_kernel, (((0,), (0,)), ((), ())), preferred_e...  20.5 us
  transfers between devices with their start and end apart: 2, of which 1 were waited for; matrix products, arithmetic and copies ran while one was open for 1% of the time, Pallas kernels for 0%

commit v1 on v0

--- a/solution.py
+++ b/solution.py
@@ -36,7 +36,9 @@
 
 def shards(query_points, cotangent, slab_ids, rel_cells, offsets, latent, w_in, b_in, w_out, b_out):
     channels = latent.shape[1]
-    slab_feats = lax.all_gather(latent, PB, axis=2, tiled=True)[0]
+    slab_feats = jnp.concatenate(
+        lax.all_to_all(jnp.stack([latent] * lax.axis_size(PB)), PB, 0, 0), axis=2
+    )[0]
     cells_slab = slab_feats.shape[1]
     slab_here = lax.axis_index("ga")
     queries_dev = query_points.shape[1]

time: 581 us -> 543 us (0.935)
  waiting for transfers between devices: 86.8 us -> 36.1 us
  starting transfers between devices: 6.81 us -> 35.3 us
  between operations: 14.1 us -> 0.77 us
    all_gather x1 -> x0, waiting for transfers between devices: 86.1 us -> none  [shards(): slab_feats = lax.all_gather(latent, PB, axis=2, tiled=True)[0]]
    all_to_all x0 -> x1, waiting for transfers between devices: none -> 36.1 us  [shards(): lax.all_to_all(jnp.stack([latent] * lax.axis_size(PB)), PB, 0, 0)]
    all_to_all x0 -> x1, starting transfers between devices: none -> 14.8 us  [shards(): lax.all_to_all(jnp.stack([latent] * lax.axis_size(PB)), PB, 0, 0)]
    all_to_all x1, starting transfers between devices: 6.78 us -> 20.6 us  [sum_at_owner(): lax.all_to_all(tiles, axis, split_axis=0, concat_axis=0, tiled=True)]
    dynamic_slice x16, local copies, waits for them, and re-layouts: 12.7 us -> 6.02 us  [shards(): lax.scan(advance, (start_grid, start_totals), inputs_all)]
where the time goes in v1:
time: 543 us; the launch traced here: 538 us
  local copies, waits for them, and re-layouts  154 us (28%)
  matrix products  111 us (20%)
  blocking collectives  89.3 us (16%)
  loops' own time  63.6 us (12%)
  other arithmetic  46.9 us (9%)
  waiting for transfers between devices  36.1 us (7%)
  starting transfers between devices  35.3 us (7%)
    psum x5, blocking collectives, by_axis(): return functools.reduce(lax.psum, axes, value)  89.3 us
    gather x96, local copies, waits for them, and re-layouts  70.8 us
    another operation x1, loops' own time, shards(): lax.scan(advance, (start_grid, start_totals), inputs_all)  62.9 us
    dynamic_update_slice x32, local copies, waits for them, and re-layouts, advance(): lax.dynamic_update_slice_in_dim(partial_grad, current + results[0][number...  59.2 us
    dot_general x8, matrix products, tile_work(): jnp.dot(w_in, features_in, precision=lax.Precision.HIGHEST, preferred_ele...  42.9 us
    all_to_all x1, waiting for transfers between devices, shards(): lax.all_to_all(jnp.stack([latent] * lax.axis_size(PB)), PB, 0, 0)  36.1 us
    add x32, other arithmetic, advance(): current + results[0][number]  32.9 us
    all_to_all x1, starting transfers between devices, sum_at_owner(): lax.all_to_all(tiles, axis, split_axis=0, concat_axis=0, tiled=True)  20.6 us
  transfers between devices with their start and end apart: 2, of which 1 were waited for; matrix products, arithmetic and copies ran while one was open for 1% of the time, Pallas kernels for 0%

profile of v1, /device:TPU:2, one launch (start us, length us, event | category | flops | bytes accessed | tf_op | source)
XLA Modules:
  0.0 537.9 jit_solution(9319520927709773844)
XLA Ops:
  3.0 14.8 %all-to-all-start = ((bf16[64,1,64,256]{3,2,1,0:T(8,128)(2,1)}), bf16[64,1,64,256]{3,2,1,0:T(8,128)(2,1)S(1)}, u32[]{:S(2)}, u32[]{:S(2)}) async-start(bf16[64,1,64,256]{3,2,1,0:T(8,128)(2,1)} %stack.8), calls=%async_computation | async-start | bytes 4194304 | tf_op jit(solution)/shard_map/all_to_all | solution.py:40
  19.5 36.1 %all-to-all-done = bf16[64,1,64,256]{3,2,1,0:T(8,128)(2,1)S(1)} async-done(((bf16[64,1,64,256]{3,2,1,0:T(8,128)(2,1)}), bf16[64,1,64,256]{3,2,1,0:T(8,128)(2,1)S(1)}, u32[]{:S(2)}, u32[]{:S(2)}) %all-to-all-start) | async-done | bytes 2097184 | tf_op jit(solution)/shard_map/all_to_all | solution.py:40
  59.4 359.9 %while.26 = (s32[]{:T(128)}, f32[64,16384]{1,0:T(8,128)}, f32[80,6]{0,1:T(8,128)S(1)}, f32[80]{0:T(128)S(1)}, f32[64,80]{1,0:T(8,128)S(1)}, /*index=5*/f32[64]{0...) while((s32[]{:T(128)}, f32[64,16384]{1,0:T(8,128)}, ...), condition=%wide.region_3.4_spmd.clone, body=%wide.region_0.3_spmd.clone.sunk | while | flops 747289728 | bytes 25849020 | solution.py:138
  69.7 8.9 %while.27 = (s32[]{:T(128)}, bf16[64,16384]{1,0:T(8,128)(2,1)}, s32[4,2]{0,1:T(2,128)S(1)}, bf16[4,64,512]{2,1,0:T(8,128)(2,1)S(1)}, s32[]{:T(128)}) while((s32[]{:T(128)}, bf16[64,16384]{1,0:T(8,128)(2,1)}, s32[4,2]{0,1:T(2,128)S(1)}, bf16[4,64,512]{2,1,0:T(8,128)(2,1)S(1)}, s32[]{:T(128)}) %tuple.83), condition=%wide.while_cond, body=%wide.while_body.sunk | while | flops 2 | bytes 131177 | solution.py:55
  81.1 5.4 fusion.121
  88.8 2.6 fusion.128
  114.7 8.9 %while.27 = (s32[]{:T(128)}, bf16[64,16384]{1,0:T(8,128)(2,1)}, s32[4,2]{0,1:T(2,128)S(1)}, bf16[4,64,512]{2,1,0:T(8,128)(2,1)S(1)}, s32[]{:T(128)}) while((s32[]{:T(128)}, bf16[64,16384]{1,0:T(8,128)(2,1)}, s32[4,2]{0,1:T(2,128)S(1)}, bf16[4,64,512]{2,1,0:T(8,128)(2,1)S(1)}, s32[]{:T(128)}) %tuple.83), condition=%wide.while_cond, body=%wide.while_body.sunk | while | flops 2 | bytes 131177 | solution.py:55
  126.1 5.4 fusion.121
  133.8 2.6 fusion.128
  159.7 8.9 %while.27 = (s32[]{:T(128)}, bf16[64,16384]{1,0:T(8,128)(2,1)}, s32[4,2]{0,1:T(2,128)S(1)}, bf16[4,64,512]{2,1,0:T(8,128)(2,1)S(1)}, s32[]{:T(128)}) while((s32[]{:T(128)}, bf16[64,16384]{1,0:T(8,128)(2,1)}, s32[4,2]{0,1:T(2,128)S(1)}, bf16[4,64,512]{2,1,0:T(8,128)(2,1)S(1)}, s32[]{:T(128)}) %tuple.83), condition=%wide.while_cond, body=%wide.while_body.sunk | while | flops 2 | bytes 131177 | solution.py:55
  171.1 5.4 fusion.121
  178.8 2.6 fusion.128
  204.7 8.9 %while.27 = (s32[]{:T(128)}, bf16[64,16384]{1,0:T(8,128)(2,1)}, s32[4,2]{0,1:T(2,128)S(1)}, bf16[4,64,512]{2,1,0:T(8,128)(2,1)S(1)}, s32[]{:T(128)}) while((s32[]{:T(128)}, bf16[64,16384]{1,0:T(8,128)(2,1)}, s32[4,2]{0,1:T(2,128)S(1)}, bf16[4,64,512]{2,1,0:T(8,128)(2,1)S(1)}, s32[]{:T(128)}) %tuple.83), condition=%wide.while_cond, body=%wide.while_body.sunk | while | flops 2 | bytes 131177 | solution.py:55
  216.1 5.4 fusion.121
  223.8 2.6 fusion.128
  249.7 8.9 %while.27 = (s32[]{:T(128)}, bf16[64,16384]{1,0:T(8,128)(2,1)}, s32[4,2]{0,1:T(2,128)S(1)}, bf16[4,64,512]{2,1,0:T(8,128)(2,1)S(1)}, s32[]{:T(128)}) while((s32[]{:T(128)}, bf16[64,16384]{1,0:T(8,128)(2,1)}, s32[4,2]{0,1:T(2,128)S(1)}, bf16[4,64,512]{2,1,0:T(8,128)(2,1)S(1)}, s32[]{:T(128)}) %tuple.83), condition=%wide.while_cond, body=%wide.while_body.sunk | while | flops 2 | bytes 131177 | solution.py:55
  261.1 5.4 fusion.121
  268.8 2.6 fusion.128
  294.7 8.9 %while.27 = (s32[]{:T(128)}, bf16[64,16384]{1,0:T(8,128)(2,1)}, s32[4,2]{0,1:T(2,128)S(1)}, bf16[4,64,512]{2,1,0:T(8,128)(2,1)S(1)}, s32[]{:T(128)}) while((s32[]{:T(128)}, bf16[64,16384]{1,0:T(8,128)(2,1)}, s32[4,2]{0,1:T(2,128)S(1)}, bf16[4,64,512]{2,1,0:T(8,128)(2,1)S(1)}, s32[]{:T(128)}) %tuple.83), condition=%wide.while_cond, body=%wide.while_body.sunk | while | flops 2 | bytes 131177 | solution.py:55
  306.1 5.4 fusion.121
  313.8 2.6 fusion.128
  339.7 8.9 %while.27 = (s32[]{:T(128)}, bf16[64,16384]{1,0:T(8,128)(2,1)}, s32[4,2]{0,1:T(2,128)S(1)}, bf16[4,64,512]{2,1,0:T(8,128)(2,1)S(1)}, s32[]{:T(128)}) while((s32[]{:T(128)}, bf16[64,16384]{1,0:T(8,128)(2,1)}, s32[4,2]{0,1:T(2,128)S(1)}, bf16[4,64,512]{2,1,0:T(8,128)(2,1)S(1)}, s32[]{:T(128)}) %tuple.83), condition=%wide.while_cond, body=%wide.while_body.sunk | while | flops 2 | bytes 131177 | solution.py:55
  351.1 5.4 fusion.121
  384.6 8.9 %while.27 = (s32[]{:T(128)}, bf16[64,16384]{1,0:T(8,128)(2,1)}, s32[4,2]{0,1:T(2,128)S(1)}, bf16[4,64,512]{2,1,0:T(8,128)(2,1)S(1)}, s32[]{:T(128)}) while((s32[]{:T(128)}, bf16[64,16384]{1,0:T(8,128)(2,1)}, s32[4,2]{0,1:T(2,128)S(1)}, bf16[4,64,512]{2,1,0:T(8,128)(2,1)S(1)}, s32[]{:T(128)}) %tuple.83), condition=%wide.while_cond, body=%wide.while_body.sunk | while | flops 2 | bytes 131177 | solution.py:55
  396.1 5.4 fusion.121
  403.7 2.6 fusion.128
  424.8 20.6 %all-to-all-start.1 = ((bf16[64,64,256]{2,1,0:T(8,128)(2,1)}), bf16[64,64,256]{2,1,0:T(8,128)(2,1)S(1)}, u32[]{:S(2)}, u32[]{:S(2)}) async-start(bf16[64,64,256]{2,1,0:T(8,128)(2,1)} %copy.33), calls=%async_computation.1 | async-start | bytes 4194304 | tf_op jit(solution)/shard_map/all_to_all | solution.py:25
  445.4 29.7 %all-reduce.3 = (f32[80,6]{0,1:T(8,128)S(1)}, f32[80]{0:T(128)S(1)}, f32[64,80]{1,0:T(8,128)S(1)}, f32[64]{0:T(128)S(1)}) all-reduce(f32[80,6]{0,1:T(8,128)S(1)} %get-tuple-element.285, f32[80]{0:T(128)S(1)} %get-tuple-element.286, ...), channel_id=1, replica_groups=mesh['pb_0'=4,'pb_1'=4,'pb_2'=2,'pb_3'=2,'ga'=4] {'pb_0'}, use_global_device_ids=true, to_apply=%region_5.6 | all-reduce | flops 5744 | bytes 45952 | tf_op jit(solution)/shard_map/psum | solution.py:30
  475.0 17.7 %all-reduce.2 = (f32[80,6]{0,1:T(8,128)S(1)}, f32[80]{0:T(128)S(1)}, f32[64,80]{1,0:T(8,128)S(1)}, f32[64]{0:T(128)S(1)}) all-reduce(f32[80,6]{0,1:T(8,128)S(1)} %get-tuple-element.497, f32[80]{0:T(128)S(1)} %get-tuple-element.498, ...), channel_id=1, replica_groups=mesh['pb_0'=4,'pb_1'=4,'pb_2'=2,'pb_3'=2,'ga'=4] {'pb_1'}, use_global_device_ids=true, to_apply=%region_6.7 | all-reduce | flops 5744 | bytes 45952 | tf_op jit(solution)/shard_map/psum | solution.py:30
  492.7 20.5 %all-reduce.5 = (f32[80,6]{0,1:T(8,128)S(1)}, f32[80]{0:T(128)S(1)}, f32[64,80]{1,0:T(8,128)S(1)}, f32[64]{0:T(128)S(1)}) all-reduce(f32[80,6]{0,1:T(8,128)S(1)} %get-tuple-element.493, f32[80]{0:T(128)S(1)} %get-tuple-element.494, ...), channel_id=1, replica_groups=mesh['pb_0'=4,'pb_1'=4,'pb_2'=2,'pb_3'=2,'ga'=4] {'pb_2'}, use_global_device_ids=true, to_apply=%region_7.8 | all-reduce | flops 5744 | bytes 45952 | tf_op jit(solution)/shard_map/psum | solution.py:30
  513.3 3.5 all-reduce.4
  516.7 17.9 %all-reduce.1 = (f32[80,6]{0,1:T(8,128)S(1)}, f32[80]{0:T(128)S(1)}, f32[64,80]{1,0:T(8,128)S(1)}, f32[64]{0:T(128)S(1)}) all-reduce(f32[80,6]{0,1:T(8,128)S(1)} %get-tuple-element.501, f32[80]{0:T(128)S(1)} %get-tuple-element.502, ...), channel_id=1, replica_groups=mesh['pb_0'=4,'pb_1'=4,'pb_2'=2,'pb_3'=2,'ga'=4] {'ga'}, use_global_device_ids=true, to_apply=%region_9.10 | all-reduce | flops 5744 | bytes 45952 | tf_op jit(solution)/shard_map/psum | solution.py:30
  (428 shorter events, 252.0 us)
Async XLA Ops:
  3.0 15.4 %copy-start.6 = (s32[1,32]{1,0:T(1,128)S(1)}, s32[1,32]{1,0:T(1,128)}, u32[]{:S(2)}) copy-start(s32[1,32]{1,0:T(1,128)} %param.16) | copy-start | bytes 388
  3.0 16.1 %copy-start.3 = (f32[3,4096]{1,0:T(4,128)S(1)}, f32[3,4096]{1,0:T(4,128)}, u32[]{:S(2)}) copy-start(f32[3,4096]{1,0:T(4,128)} %param.12) | copy-start | bytes 147460
  3.0 16.2 %copy-start.2 = (bf16[64,4096]{1,0:T(8,128)(2,1)S(1)}, bf16[64,4096]{1,0:T(8,128)(2,1)}, u32[]{:S(2)}) copy-start(bf16[64,4096]{1,0:T(8,128)(2,1)} %param.13) | copy-start | bytes 1572868
  3.0 52.7 %all-to-all-start = ((bf16[64,1,64,256]{3,2,1,0:T(8,128)(2,1)}), bf16[64,1,64,256]{3,2,1,0:T(8,128)(2,1)S(1)}, u32[]{:S(2)}, u32[]{:S(2)}) async-start(bf16[64,1,64,256]{3,2,1,0:T(8,128)(2,1)} %stack.8), calls=%async_computation | async-start | bytes 4194304 | tf_op jit(solution)/shard_map/all_to_all | solution.py:40
  57.1 2.3 copy-start.4
  57.1 2.3 copy-start.5
  57.1 2.3 copy-start.7
  57.1 2.3 copy-start.8
  59.4 19.2 %copy-start = (bf16[8,4,64,128]{3,1,0,2:T(4,128)(2,1)}, bf16[8,4,64,128]{3,1,0,2:T(4,128)(2,1)S(1)}, u32[]{:S(2)}) copy-start(bf16[8,4,64,128]{3,1,0,2:T(4,128)(2,1)S(1)} %get-tuple-element.781) | copy-start | bytes 1572868 | tf_op jit(solution)/shard_map/while
  92.9 11.6 %copy-start.1 = (bf16[8,4,64,128]{3,1,0,2:T(4,128)(2,1)S(1)}, bf16[8,4,64,128]{3,1,0,2:T(4,128)(2,1)}, u32[]{:S(2)}) copy-start(bf16[8,4,64,128]{3,1,0,2:T(4,128)(2,1)} %copy-done) | copy-start | bytes 1572868 | tf_op jit(solution)/shard_map/while
  104.5 19.2 %copy-start = (bf16[8,4,64,128]{3,1,0,2:T(4,128)(2,1)}, bf16[8,4,64,128]{3,1,0,2:T(4,128)(2,1)S(1)}, u32[]{:S(2)}) copy-start(bf16[8,4,64,128]{3,1,0,2:T(4,128)(2,1)S(1)} %get-tuple-element.781) | copy-start | bytes 1572868 | tf_op jit(solution)/shard_map/while
  137.9 11.6 %copy-start.1 = (bf16[8,4,64,128]{3,1,0,2:T(4,128)(2,1)S(1)}, bf16[8,4,64,128]{3,1,0,2:T(4,128)(2,1)}, u32[]{:S(2)}) copy-start(bf16[8,4,64,128]{3,1,0,2:T(4,128)(2,1)} %copy-done) | copy-start | bytes 1572868 | tf_op jit(solution)/shard_map/while
  149.5 19.2 %copy-start = (bf16[8,4,64,128]{3,1,0,2:T(4,128)(2,1)}, bf16[8,4,64,128]{3,1,0,2:T(4,128)(2,1)S(1)}, u32[]{:S(2)}) copy-start(bf16[8,4,64,128]{3,1,0,2:T(4,128)(2,1)S(1)} %get-tuple-element.781) | copy-start | bytes 1572868 | tf_op jit(solution)/shard_map/while
  182.9 11.5 %copy-start.1 = (bf16[8,4,64,128]{3,1,0,2:T(4,128)(2,1)S(1)}, bf16[8,4,64,128]{3,1,0,2:T(4,128)(2,1)}, u32[]{:S(2)}) copy-start(bf16[8,4,64,128]{3,1,0,2:T(4,128)(2,1)} %copy-done) | copy-start | bytes 1572868 | tf_op jit(solution)/shard_map/while
  194.4 19.2 %copy-start = (bf16[8,4,64,128]{3,1,0,2:T(4,128)(2,1)}, bf16[8,4,64,128]{3,1,0,2:T(4,128)(2,1)S(1)}, u32[]{:S(2)}) copy-start(bf16[8,4,64,128]{3,1,0,2:T(4,128)(2,1)S(1)} %get-tuple-element.781) | copy-start | bytes 1572868 | tf_op jit(solution)/shard_map/while
  227.8 11.6 %copy-start.1 = (bf16[8,4,64,128]{3,1,0,2:T(4,128)(2,1)S(1)}, bf16[8,4,64,128]{3,1,0,2:T(4,128)(2,1)}, u32[]{:S(2)}) copy-start(bf16[8,4,64,128]{3,1,0,2:T(4,128)(2,1)} %copy-done) | copy-start | bytes 1572868 | tf_op jit(solution)/shard_map/while
  239.4 19.2 %copy-start = (bf16[8,4,64,128]{3,1,0,2:T(4,128)(2,1)}, bf16[8,4,64,128]{3,1,0,2:T(4,128)(2,1)S(1)}, u32[]{:S(2)}) copy-start(bf16[8,4,64,128]{3,1,0,2:T(4,128)(2,1)S(1)} %get-tuple-element.781) | copy-start | bytes 1572868 | tf_op jit(solution)/shard_map/while
  272.9 11.6 %copy-start.1 = (bf16[8,4,64,128]{3,1,0,2:T(4,128)(2,1)S(1)}, bf16[8,4,64,128]{3,1,0,2:T(4,128)(2,1)}, u32[]{:S(2)}) copy-start(bf16[8,4,64,128]{3,1,0,2:T(4,128)(2,1)} %copy-done) | copy-start | bytes 1572868 | tf_op jit(solution)/shard_map/while
  284.5 19.2 %copy-start = (bf16[8,4,64,128]{3,1,0,2:T(4,128)(2,1)}, bf16[8,4,64,128]{3,1,0,2:T(4,128)(2,1)S(1)}, u32[]{:S(2)}) copy-start(bf16[8,4,64,128]{3,1,0,2:T(4,128)(2,1)S(1)} %get-tuple-element.781) | copy-start | bytes 1572868 | tf_op jit(solution)/shard_map/while
  317.9 11.6 %copy-start.1 = (bf16[8,4,64,128]{3,1,0,2:T(4,128)(2,1)S(1)}, bf16[8,4,64,128]{3,1,0,2:T(4,128)(2,1)}, u32[]{:S(2)}) copy-start(bf16[8,4,64,128]{3,1,0,2:T(4,128)(2,1)} %copy-done) | copy-start | bytes 1572868 | tf_op jit(solution)/shard_map/while
  329.4 19.2 %copy-start = (bf16[8,4,64,128]{3,1,0,2:T(4,128)(2,1)}, bf16[8,4,64,128]{3,1,0,2:T(4,128)(2,1)S(1)}, u32[]{:S(2)}) copy-start(bf16[8,4,64,128]{3,1,0,2:T(4,128)(2,1)S(1)} %get-tuple-element.781) | copy-start | bytes 1572868 | tf_op jit(solution)/shard_map/while
  362.8 11.5 %copy-start.1 = (bf16[8,4,64,128]{3,1,0,2:T(4,128)(2,1)S(1)}, bf16[8,4,64,128]{3,1,0,2:T(4,128)(2,1)}, u32[]{:S(2)}) copy-start(bf16[8,4,64,128]{3,1,0,2:T(4,128)(2,1)} %copy-done) | copy-start | bytes 1572868 | tf_op jit(solution)/shard_map/while
  374.4 19.2 %copy-start = (bf16[8,4,64,128]{3,1,0,2:T(4,128)(2,1)}, bf16[8,4,64,128]{3,1,0,2:T(4,128)(2,1)S(1)}, u32[]{:S(2)}) copy-start(bf16[8,4,64,128]{3,1,0,2:T(4,128)(2,1)S(1)} %get-tuple-element.781) | copy-start | bytes 1572868 | tf_op jit(solution)/shard_map/while
  407.8 11.5 %copy-start.1 = (bf16[8,4,64,128]{3,1,0,2:T(4,128)(2,1)S(1)}, bf16[8,4,64,128]{3,1,0,2:T(4,128)(2,1)}, u32[]{:S(2)}) copy-start(bf16[8,4,64,128]{3,1,0,2:T(4,128)(2,1)} %copy-done) | copy-start | bytes 1572868 | tf_op jit(solution)/shard_map/while
  424.8 112.1 %all-to-all-start.1 = ((bf16[64,64,256]{2,1,0:T(8,128)(2,1)}), bf16[64,64,256]{2,1,0:T(8,128)(2,1)S(1)}, u32[]{:S(2)}, u32[]{:S(2)}) async-start(bf16[64,64,256]{2,1,0:T(8,128)(2,1)} %copy.33), calls=%async_computation.1 | async-start | bytes 4194304 | tf_op jit(solution)/shard_map/all_to_all | solution.py:25
